TPU v7x, 256 devices: a whole 4x4x8 slice. The times are simulated.
256 devices in a mesh: dp: 8 (over x, core), mp: 32 (over y, z).
Axes of the slice: x: 4, y: 4, z: 8, core: 2. Of those that a mesh axis runs over, the one named last changes fastest.
Arguments:
- hidden: bfloat16 [8, 4, 512, 2048], P('dp', None, None, 'mp'), may hold values from -6 to 6
- gain: float32 [2048], P('mp'), may hold values from 0.1 to 1.9
- cotangent: bfloat16 [8, 4, 512, 2048], P('dp', None, None, 'mp'), may hold values from -600 to 600
- blocks: int32 [8, 4, 2], P('dp'), may hold values from 1 to 2
- loss_mask: int32 [8, 4, 512], P('dp'), may hold values 0 or 1
- wi_gate: bfloat16 [5120, 2048], P('mp'), may hold values from -0.125 to 0.125
- wi_up: bfloat16 [5120, 2048], P('mp'), may hold values from -0.125 to 0.125
- wo_weight: bfloat16 [5120, 2048], P('mp'), may hold values from -0.078125 to 0.078125
Outputs:
- gradients: float32 [3, 5120, 2048], P(None, 'mp')
Inputs may be any that keep to these rules, and one draw needn't show every extreme that they name: blocks of 128 target positions used by a sequence; later positions are padding.
All inputs are finite; a program needn't handle non-finite values. No bound on the sum of `loss_mask` on one device may be relied on, other than what follows from the above.
Results may differ from a plain program's by a relative error of at most 0.0059.
Values may be sent and summed in bfloat16 or wider, within the bound.
No kernel may reach another device: no remote copies, remote signals or barrier semaphores. Data moves between devices by JAX's collectives and lax.ppermute only.
A program may use at most 128 MiB of HBM per device.

v0:
```python
import jax
import jax.numpy as jnp
from jax import lax
from jax.sharding import PartitionSpec as P

D = 2048
BLOCK = 128
TLEN = 256


def sent_to_all(x, axis):
    devices = lax.axis_size(axis)
    return lax.all_to_all(jnp.broadcast_to(x[None], (devices, *x.shape)), axis, 0, 0, tiled=True)


def over_copies(x, axis):
    return sent_to_all(x, axis).sum(axis=0)


def gather_turned(arrays, axis, dims):
    turned = [jnp.moveaxis(a, dim, 0) for a, dim in zip(arrays, dims)]
    widths = [t[0].size for t in turned]
    both = jnp.concatenate([t.reshape(-1, w) for t, w in zip(turned, widths)], axis=1)
    out = lax.all_gather(both, axis, axis=0, tiled=True)
    blocks = jnp.split(out, [sum(widths[:k]) for k in range(1, len(widths))], axis=1)
    return tuple(
        (
            jnp.moveaxis(b.reshape(-1, *t.shape[1:]), 0, dim)
            for b, t, dim in zip(blocks, turned, dims)
        )
    )


def in_blocks(x, dim, devices):
    lengths = x.shape
    blocks = x.reshape(*lengths[:dim], devices, lengths[dim] // devices, *lengths[dim + 1 :])
    return jnp.moveaxis(blocks, dim, 0)


def summed_on_arrival(x, axis, dim):
    blocks = in_blocks(x, dim, lax.axis_size(axis))
    arrived = lax.all_to_all(blocks, axis, split_axis=0, concat_axis=0, tiled=True)
    return arrived.astype(jnp.float32).sum(axis=0)


def gelu_tanh(value):
    return jax.nn.gelu(value, approximate=True)


def contributions(normed, tangent, wi_gate, wi_up, wo_weight):
    rows_dims = (((1,), (1,)), ((), ()))
    gate_pre = lax.dot_general(normed, wi_gate, rows_dims, preferred_element_type=jnp.float32)
    up_pre = lax.dot_general(normed, wi_up, rows_dims, preferred_element_type=jnp.float32)
    activated, pullback = jax.vjp(gelu_tanh, gate_pre)
    inner = (activated * up_pre).astype(jnp.bfloat16)
    back_grad = lax.dot_general(tangent, wo_weight, rows_dims, preferred_element_type=jnp.float32)
    grad_gate = pullback(back_grad * up_pre)[0].astype(jnp.bfloat16)
    grad_up = (back_grad * activated).astype(jnp.bfloat16)
    dims = (((0,), (0,)), ((), ()))
    first_grad = lax.dot_general(grad_gate, normed, dims, preferred_element_type=jnp.float32)
    second_grad = lax.dot_general(grad_up, normed, dims, preferred_element_type=jnp.float32)
    third_grad = lax.dot_general(inner, tangent, dims, preferred_element_type=jnp.float32)
    return jnp.stack([first_grad, second_grad, third_grad])


def on_device(hidden, gain, cotangent, blocks, loss_mask, wi_gate, wi_up, wo_weight):
    row_count = hidden.shape[2]
    micro_count = hidden.shape[1]
    position = lax.iota(jnp.int32, row_count)
    offset = position % TLEN
    sequence = position // TLEN
    picker = (sequence[None, :] == lax.iota(jnp.int32, blocks.shape[2])[:, None]).astype(jnp.int32)
    limit_pos = jnp.sum(blocks[0][:, :, None] * picker[None, :, :], axis=1) * BLOCK
    weight = (offset[None, :] < limit_pos).astype(jnp.int32) * loss_mask[0]
    token_total = over_copies(jnp.sum(weight), "dp")
    denominator = jnp.maximum(token_total, 1).astype(jnp.float32)
    states = hidden[0].astype(jnp.float32)
    squares = over_copies(jnp.sum(states * states, axis=-1), "mp")
    normed = (states * lax.rsqrt(squares / D + 1e-06)[:, :, None] * gain).astype(jnp.bfloat16)
    tangent = cotangent[0] * weight[:, :, None].astype(jnp.bfloat16)
    zeros_grad = jnp.zeros((3, wi_gate.shape[0], wi_gate.shape[1]), jnp.float32)
    running_sum = zeros_grad
    compensation = zeros_grad
    for micro_step in range(micro_count):
        whole_normed, whole_tangent = gather_turned(
            (normed[micro_step], tangent[micro_step]), "mp", (1, 1)
        )
        contrib = contributions(whole_normed, whole_tangent, wi_gate, wi_up, wo_weight)
        adjusted = contrib - compensation
        running = running_sum + adjusted
        compensation = running - running_sum - adjusted
        running_sum = running
    share_part = summed_on_arrival(running_sum.astype(jnp.bfloat16), "dp", 2)
    share_part = share_part / denominator
    result = lax.all_gather(share_part.astype(jnp.bfloat16), "dp", axis=2, tiled=True).astype(
        share_part.dtype
    )
    return result


def solution(mesh):
    return jax.shard_map(
        on_device,
        mesh=mesh,
        in_specs=(
            P("dp", None, None, "mp"),
            P("mp"),
            P("dp", None, None, "mp"),
            P("dp", None, None),
            P("dp", None, None),
            P("mp", None),
            P("mp", None),
            P("mp", None),
        ),
        out_specs=P(None, "mp", None),
        check_vma=False,
    )
```

profile of v0, /device:TPU:1, one launch (start us, length us, event | category | flops | bytes accessed | tf_op | source)
XLA Modules:
  0.0 439.2 jit_solution(2142887319784037128)
XLA Ops:
  6.5 1.1 fusion.51
  7.6 0.7 broadcast_in_dim.4
  8.4 12.0 %all-to-all-start = ((f32[32,4,512]{2,1,0:T(4,128)}), f32[32,4,512]{2,1,0:T(4,128)S(1)}, u32[]{:S(2)}, u32[]{:S(2)}) async-start(f32[32,4,512]{2,1,0:T(4,128)} %broadcast_in_dim.4), calls=%async_computation | async-start | bytes 524288 | tf_op jit(solution)/shard_map/all_to_all | solution.py:13
  20.5 0.8 multiply_reduce_fusion
  21.3 1.4 fusion.115
  22.7 1.0 bitcast_multiply_fusion
  23.6 6.5 %all-to-all-done = f32[32,4,512]{2,1,0:T(4,128)S(1)} async-done(((f32[32,4,512]{2,1,0:T(4,128)}), f32[32,4,512]{2,1,0:T(4,128)S(1)}, u32[]{:S(2)}, u32[]{:S(2)}) %all-to-all-start) | async-done | bytes 262176 | tf_op jit(solution)/shard_map/all_to_all | solution.py:13
  30.2 0.8 fusion.53
  31.0 0.7 pad_maximum_fusion.3
  31.7 0.7 pad_maximum_fusion
  32.5 0.7 pad_maximum_fusion.2
  33.2 0.7 pad_maximum_fusion.1
  33.9 1.2 broadcast_in_dim.5
  35.1 8.0 %all-to-all-start.2 = ((s32[8,1,1]{2,1,0:T(1,128)}), s32[8,1,1]{2,1,0:T(1,128)S(1)}, u32[]{:S(2)}, u32[]{:S(2)}) async-start(s32[8,1,1]{2,1,0:T(1,128)} %broadcast_in_dim.5), calls=%async_computation.2 | async-start | bytes 8192 | tf_op jit(solution)/shard_map/all_to_all | solution.py:13
  43.1 65.9 %all-gather.12.cloned.1.call-done = bf16[2048,1024]{1,0:T(8,128)(2,1)} async-done(((bf16[64,1024]{1,0:T(8,128)(2,1)}), bf16[2048,1024]{1,0:T(8,128)(2,1)}) %all-gather.12.cloned.1.call-update) | async-done | bytes 4194320 | tf_op jit(solution)/shard_map/all_gather | solution.py:24
  109.0 2.2 fusion.23
  111.3 2.1 fusion.25
  113.4 0.9 fusion.3
  114.2 0.5 copy.62
  115.3 0.5 fusion.5
  115.9 0.9 fusion.19
  116.7 0.5 copy.61
  117.6 1.0 fusion.21
  118.6 0.5 copy.60
  119.1 1.5 copy.45
  120.6 69.6 %all-gather.6.cloned.1.call-done = bf16[2048,1024]{1,0:T(8,128)(2,1)} async-done(((bf16[64,1024]{1,0:T(8,128)(2,1)}), bf16[2048,1024]{1,0:T(8,128)(2,1)}) %all-gather.6.cloned.1.call-update) | async-done | bytes 4194320 | tf_op jit(solution)/shard_map/all_gather | solution.py:24
  190.2 2.4 fusion.49
  192.6 2.3 fusion.17
  194.9 0.6 fusion.47
  195.5 1.0 fusion.45
  196.5 1.5 copy.51
  198.0 0.9 fusion.43
  198.9 1.6 copy.52
  200.5 0.9 fusion.15
  201.3 1.5 copy.53
  202.8 68.5 %all-gather.10.cloned.1.call-done = bf16[2048,1024]{1,0:T(8,128)(2,1)} async-done(((bf16[64,1024]{1,0:T(8,128)(2,1)}), bf16[2048,1024]{1,0:T(8,128)(2,1)}) %all-gather.10.cloned.1.call-update) | async-done | bytes 4194320 | tf_op jit(solution)/shard_map/all_gather | solution.py:24
  271.4 2.2 fusion.31
  273.6 2.3 fusion.33
  275.9 0.9 fusion.7
  277.3 1.7 copy.44
  279.0 0.5 fusion.9
  279.5 0.9 fusion.27
  280.3 0.5 copy.58
  280.8 1.5 copy.43
  282.3 1.0 fusion.29
  283.8 1.5 copy.42
  285.3 1.5 copy_dynamic-update-slice_fusion.2
  286.7 65.7 %all-gather.8.cloned.1.call-done = bf16[2048,1024]{1,0:T(8,128)(2,1)} async-done(((bf16[64,1024]{1,0:T(8,128)(2,1)}), bf16[2048,1024]{1,0:T(8,128)(2,1)}) %all-gather.8.cloned.1.call-update) | async-done | bytes 4194320 | tf_op jit(solution)/shard_map/all_gather | solution.py:24
  352.4 2.2 fusion.39
  354.6 2.3 fusion.41
  357.0 0.9 fusion.11
  358.9 0.5 fusion.13
  359.4 0.9 fusion.35
  360.3 0.5 copy.55
  361.2 1.0 fusion.37
  363.1 1.2 copy-done.1
  365.5 0.5 copy-done.2
  367.2 2.5 fusion.2
  369.7 8.5 %all-to-all-start.1 = ((bf16[8,3,160,256]{3,2,1,0:T(8,128)(2,1)}), bf16[8,3,160,256]{3,2,1,0:T(8,128)(2,1)S(1)}, u32[]{:S(2)}, u32[]{:S(2)}) async-start(bf16[8,3,160,256]{3,2,1,0:T(8,128)(2,1)} %fusion.2), calls=%async_computation.1 | async-start | bytes 3932160 | tf_op jit(solution)/shard_map/all_to_all | solution.py:42
  378.2 0.7 reduce_sum.59
  379.5 23.5 %all-to-all-done.1 = bf16[8,3,160,256]{3,2,1,0:T(8,128)(2,1)S(1)} async-done(((bf16[8,3,160,256]{3,2,1,0:T(8,128)(2,1)}), bf16[8,3,160,256]{3,2,1,0:T(8,128)(2,1)S(1)}, u32[]{:S(2)}, u32[]{:S(2)}) %all-to-all-start.1) | async-done | bytes 1966112 | tf_op jit(solution)/shard_map/all_to_all | solution.py:42
  403.2 0.7 divide_convert_fusion
  404.0 24.7 %all-gather.14.cloned.1.call-done = bf16[3,160,2048]{2,1,0:T(8,128)(2,1)} async-done(((bf16[3,160,256]{2,1,0:T(8,128)(2,1)}), bf16[3,160,2048]{2,1,0:T(8,128)(2,1)}) %all-gather.14.cloned.1.call-update) | async-done | bytes 1966096 | tf_op jit(solution)/shard_map/all_gather | solution.py:95
  428.7 4.0 convert_element_type.98
  (63 shorter events, 7.4 us)
Async XLA Ops:
  6.5 102.5 %copy-start = (bf16[160,2048]{1,0:T(8,128)(2,1)S(1)}, bf16[160,2048]{1,0:T(8,128)(2,1)}, u32[]{:S(2)}) copy-start(bf16[160,2048]{1,0:T(8,128)(2,1)} %param.14) | copy-start | bytes 1966084
  6.5 23.6 %copy-start.13 = (bf16[1,4,512,64]{2,3,1,0:T(8,128)(2,1)S(1)}, bf16[1,4,512,64]{2,3,1,0:T(8,128)(2,1)}, u32[]{:S(2)}) copy-start(bf16[1,4,512,64]{2,3,1,0:T(8,128)(2,1)} %param.8) | copy-start | bytes 786436
  8.4 21.7 %all-to-all-start = ((f32[32,4,512]{2,1,0:T(4,128)}), f32[32,4,512]{2,1,0:T(4,128)S(1)}, u32[]{:S(2)}, u32[]{:S(2)}) async-start(f32[32,4,512]{2,1,0:T(4,128)} %broadcast_in_dim.4), calls=%async_computation | async-start | bytes 524288 | tf_op jit(solution)/shard_map/all_to_all | solution.py:13
  20.4 88.6 %all-gather.12.cloned.1.call-start = ((), (), s32[]{:S(2)}) async-start(), calls=%async_computation.6 | async-start | bytes 4325376 | tf_op jit(solution)/shard_map/all_gather | solution.py:24
  31.7 158.5 %all-gather.6.cloned.1.call-start = ((), (), s32[]{:S(2)}) async-start(), calls=%async_computation.3 | async-start | bytes 4325376 | tf_op jit(solution)/shard_map/all_gather | solution.py:24
  32.4 238.9 %all-gather.10.cloned.1.call-start = ((), (), s32[]{:S(2)}) async-start(), calls=%async_computation.5 | async-start | bytes 4325376 | tf_op jit(solution)/shard_map/all_gather | solution.py:24
  33.1 78.1 %copy-start.14 = (bf16[160,2048]{1,0:T(8,128)(2,1)S(1)}, bf16[160,2048]{1,0:T(8,128)(2,1)}, u32[]{:S(2)}) copy-start(bf16[160,2048]{1,0:T(8,128)(2,1)} %param.13) | copy-start | bytes 1966084
  33.2 319.2 %all-gather.8.cloned.1.call-start = ((), (), s32[]{:S(2)}) async-start(), calls=%async_computation.4 | async-start | bytes 4325376 | tf_op jit(solution)/shard_map/all_gather | solution.py:24
  35.1 334.6 %all-to-all-start.2 = ((s32[8,1,1]{2,1,0:T(1,128)}), s32[8,1,1]{2,1,0:T(1,128)S(1)}, u32[]{:S(2)}, u32[]{:S(2)}) async-start(s32[8,1,1]{2,1,0:T(1,128)} %broadcast_in_dim.5), calls=%async_computation.2 | async-start | bytes 8192 | tf_op jit(solution)/shard_map/all_to_all | solution.py:13
  109.0 4.4 copy-start.12
  114.2 1.1 copy-start.15
  190.2 4.8 %copy-start.11 = (bf16[2048,1024]{1,0:T(8,128)(2,1)S(1)}, bf16[2048,1024]{1,0:T(8,128)(2,1)}, u32[]{:S(2)}) copy-start(bf16[2048,1024]{1,0:T(8,128)(2,1)} %all-gather.6.cloned.1.call-done) | copy-start | bytes 12582916
  271.4 4.6 %copy-start.10 = (bf16[2048,1024]{1,0:T(8,128)(2,1)S(1)}, bf16[2048,1024]{1,0:T(8,128)(2,1)}, u32[]{:S(2)}) copy-start(bf16[2048,1024]{1,0:T(8,128)(2,1)} %all-gather.10.cloned.1.call-done) | copy-start | bytes 12582916
  276.8 2.2 copy-start.16
  283.3 2.0 copy-start.8
  352.4 4.6 %copy-start.9 = (bf16[2048,1024]{1,0:T(8,128)(2,1)S(1)}, bf16[2048,1024]{1,0:T(8,128)(2,1)}, u32[]{:S(2)}) copy-start(bf16[2048,1024]{1,0:T(8,128)(2,1)} %all-gather.8.cloned.1.call-done) | copy-start | bytes 12582916
  357.8 1.1 copy-start.17
  361.2 3.9 copy-start.7
  362.2 2.1 copy-start.1
  362.2 2.5 copy-start.6
  364.7 1.3 copy-start.2
  364.7 1.7 copy-start.3
  364.7 2.1 copy-start.4
  364.7 2.5 copy-start.5
  369.7 33.3 %all-to-all-start.1 = ((bf16[8,3,160,256]{3,2,1,0:T(8,128)(2,1)}), bf16[8,3,160,256]{3,2,1,0:T(8,128)(2,1)S(1)}, u32[]{:S(2)}, u32[]{:S(2)}) async-start(bf16[8,3,160,256]{3,2,1,0:T(8,128)(2,1)} %fusion.2), calls=%async_computation.1 | async-start | bytes 3932160 | tf_op jit(solution)/shard_map/all_to_all | solution.py:42
  378.2 50.6 %all-gather.14.cloned.1.call-start = ((), (), s32[]{:S(2)}) async-start(), calls=%async_computation.7 | async-start | bytes 2211840 | tf_op jit(solution)/shard_map/all_gather | solution.py:95
Sparse Core Ops, SparseCore 0:
  31.8 77.1 all-gather.11
  111.6 78.5 all-gather.5
  192.8 78.5 all-gather.9
  273.8 78.5 all-gather.7
  404.1 24.5 all-gather.13
where the time goes:
time: 440 us; the launch traced here: 439 us
  waiting for transfers between devices  324 us (74%)
  matrix products  31 us (7%)
  starting transfers between devices  28.7 us (7%)
  local copies, waits for them, and re-layouts  25.1 us (6%)
  other arithmetic  15.9 us (4%)
  between operations  14.2 us (3%)
    all_gather x4, waiting for transfers between devices, gather_turned(): out = lax.all_gather(both, axis, axis=0, tiled=True)  270 us
    all_gather x1, waiting for transfers between devices, on_device(): lax.all_gather(share_part.astype(jnp.bfloat16), 'dp', axis=2, tiled=True)  24.7 us
    all_to_all x1, waiting for transfers between devices, summed_on_arrival(): lax.all_to_all(blocks, axis, split_axis=0, concat_axis=0, tiled=True)  23.5 us
    all_to_all x2, starting transfers between devices, sent_to_all(): lax.all_to_all(jnp.broadcast_to(x[None], (devices, *x.shape)), axis, 0, 0...  20 us
    unnamed x50, local copies, waits for them, and re-layouts  14.4 us
    dot_general x4, matrix products, contributions(): lax.dot_general(normed, wi_gate, rows_dims, preferred_element_type=jnp.fl...  9.16 us
  transfers between devices with their start and end apart: 8, of which 7 were waited for; matrix products, arithmetic and copies ran while one was open for 14% of the time, Pallas kernels for 0%

commit v1 on v0

v1 whole, which is shorter than its diff:
```python
import jax
import jax.numpy as jnp
from jax import lax
from jax.sharding import PartitionSpec as P

D = 2048
BLOCK = 128
TLEN = 256


def sent_to_all(x, axis):
    devices = lax.axis_size(axis)
    return lax.all_to_all(jnp.broadcast_to(x[None], (devices, *x.shape)), axis, 0, 0, tiled=True)


def in_blocks(x, dim, devices):
    lengths = x.shape
    blocks = x.reshape(*lengths[:dim], devices, lengths[dim] // devices, *lengths[dim + 1 :])
    return jnp.moveaxis(blocks, dim, 0)


def summed_on_arrival(x, axis, dim):
    blocks = in_blocks(x, dim, lax.axis_size(axis))
    arrived = lax.all_to_all(blocks, axis, split_axis=0, concat_axis=0, tiled=True)
    return arrived.astype(jnp.float32).sum(axis=0)


def gelu_tanh(value):
    return jax.nn.gelu(value, approximate=True)


def contributions(normed, tangent, wi_gate, wi_up, wo_weight):
    rows_dims = (((1,), (0,)), ((), ()))
    gate_pre = lax.dot_general(wi_gate, normed, rows_dims, preferred_element_type=jnp.float32)
    up_pre = lax.dot_general(wi_up, normed, rows_dims, preferred_element_type=jnp.float32)
    activated, pullback = jax.vjp(gelu_tanh, gate_pre)
    inner = (activated * up_pre).astype(jnp.bfloat16)
    back_grad = lax.dot_general(wo_weight, tangent, rows_dims, preferred_element_type=jnp.float32)
    grad_gate = pullback(back_grad * up_pre)[0].astype(jnp.bfloat16)
    grad_up = (back_grad * activated).astype(jnp.bfloat16)
    dims = (((1,), (1,)), ((), ()))
    first_grad = lax.dot_general(grad_gate, normed, dims, preferred_element_type=jnp.float32)
    second_grad = lax.dot_general(grad_up, normed, dims, preferred_element_type=jnp.float32)
    third_grad = lax.dot_general(inner, tangent, dims, preferred_element_type=jnp.float32)
    return first_grad, second_grad, third_grad


def on_device(hidden, gain, cotangent, blocks, loss_mask, wi_gate, wi_up, wo_weight):
    row_count = hidden.shape[2]
    micro_count = hidden.shape[1]
    own = jnp.concatenate(
        [jnp.moveaxis(a[0], 2, 0).reshape(a.shape[3], -1) for a in (hidden, cotangent)], axis=1
    )
    whole = lax.all_gather(own, "mp", axis=0, tiled=True)
    whole_gain = sent_to_all(gain, "mp").reshape(-1, 1)
    position = lax.iota(jnp.int32, row_count)
    offset = position % TLEN
    sequence = position // TLEN
    picker = (sequence[None, :] == lax.iota(jnp.int32, blocks.shape[2])[:, None]).astype(jnp.int32)
    limit_pos = jnp.sum(blocks[0][:, :, None] * picker[None, :, :], axis=1) * BLOCK
    weight = (offset[None, :] < limit_pos).astype(jnp.int32) * loss_mask[0]
    token_total = sent_to_all(jnp.sum(weight), "dp").sum(axis=0)
    denominator = jnp.maximum(token_total, 1).astype(jnp.float32)
    totals = [jnp.zeros(wi_gate.shape, jnp.float32)] * 3
    comps = totals
    for micro_step in range(micro_count):
        start = micro_step * row_count
        states = whole[:, start : start + row_count].astype(jnp.float32)
        squares = jnp.sum(states * states, axis=0, keepdims=True)
        normed = (states * lax.rsqrt(squares / D + 1e-06) * whole_gain).astype(jnp.bfloat16)
        start += micro_count * row_count
        tangent = whole[:, start : start + row_count] * weight[micro_step][None].astype(jnp.bfloat16)
        terms = contributions(normed, tangent, wi_gate, wi_up, wo_weight)
        adjusted = [term - comp for term, comp in zip(terms, comps)]
        running = [total + a for total, a in zip(totals, adjusted)]
        comps = [r - total - a for r, total, a in zip(running, totals, adjusted)]
        totals = running
    running_sum = jnp.stack([total.astype(jnp.bfloat16) for total in totals])
    share_part = summed_on_arrival(running_sum, "dp", 2)
    share_part = share_part / denominator
    result = lax.all_gather(share_part.astype(jnp.bfloat16), "dp", axis=2, tiled=True).astype(
        share_part.dtype
    )
    return result


def solution(mesh):
    return jax.shard_map(
        on_device,
        mesh=mesh,
        in_specs=(
            P("dp", None, None, "mp"),
            P("mp"),
            P("dp", None, None, "mp"),
            P("dp", None, None),
            P("dp", None, None),
            P("mp", None),
            P("mp", None),
            P("mp", None),
        ),
        out_specs=P(None, "mp", None),
        check_vma=False,
    )
```

time: 440 us -> 251 us (0.57)
  waiting for transfers between devices: 324 us -> 169 us
  local copies, waits for them, and re-layouts: 25.1 us -> 6.47 us
  matrix products: 31 us -> 20.2 us
  starting transfers between devices: 28.7 us -> 24.1 us
    all_gather x4 -> x1, waiting for transfers between devices: 270 us -> 113 us  [on_device(): whole = lax.all_gather(own, 'mp', axis=0, tiled=True)]
    unnamed x50 -> x17, local copies, waits for them, and re-layouts: 14.4 us -> 1.51 us
    dot_general x12, matrix products: 20.3 us -> 7.51 us  [the longest x4 2.69 us: contributions(): lax.dot_general(wi_gate, normed, rows_dims, preferred_element_type=jnp.fl...]
    another operation x10 -> x3, local copies, waits for them, and re-layouts: 8.64 us -> 0.38 us  [on_device(): running_sum = jnp.stack([total.astype(jnp.bfloat16) for total in totals])]
  transfers between devices with their start and end apart: 8 -> 5, of which waited for: 7 -> 4; matrix products, arithmetic and copies ran while one was open for 14% -> 14% of each run, Pallas kernels for 0% -> 0%
where the time goes in v1:
time: 251 us
  waiting for transfers between devices  169 us (67%)
  starting transfers between devices  24.1 us (10%)
  matrix products  20.2 us (8%)
  other arithmetic  16.7 us (7%)
  between operations  14.4 us (6%)
  local copies, waits for them, and re-layouts  6.47 us (3%)
    all_gather x1, waiting for transfers between devices, on_device(): whole = lax.all_gather(own, 'mp', axis=0, tiled=True)  113 us
    all_gather x1, waiting for transfers between devices, on_device(): lax.all_gather(share_part.astype(jnp.bfloat16), 'dp', axis=2, tiled=True)  25 us
    all_to_all x1, waiting for transfers between devices, summed_on_arrival(): lax.all_to_all(blocks, axis, split_axis=0, concat_axis=0, tiled=True)  23.4 us
    all_to_all x2, starting transfers between devices, sent_to_all(): lax.all_to_all(jnp.broadcast_to(x[None], (devices, *x.shape)), axis, 0, 0...  18.4 us
    all_to_all x2, waiting for transfers between devices, sent_to_all(): lax.all_to_all(jnp.broadcast_to(x[None], (devices, *x.shape)), axis, 0, 0...  7.79 us
    all_to_all x1, starting transfers between devices, summed_on_arrival(): lax.all_to_all(blocks, axis, split_axis=0, concat_axis=0, tiled=True)  5.65 us
  transfers between devices with their start and end apart: 5, of which 4 were waited for; matrix products, arithmetic and copies ran while one was open for 14% of the time, Pallas kernels for 0%

profile of v1, /device:TPU:1, one launch (start us, length us, event | category | flops | bytes accessed | tf_op | source)
XLA Modules:
  0.0 251.0 jit_solution(16214452360944582158)
XLA Ops:
  6.5 0.0 copy-start
  6.5 0.0 all-gather.3.cloned.1.call-start
  6.6 1.0 copy.31
  7.6 1.0 copy.32
  8.6 0.8 pad_maximum_fusion
  9.4 0.0 all-gather.3.cloned.1.call-update
  9.4 0.0 copy-done.5
  9.5 0.0 copy-start.2
  9.5 0.6 broadcast_in_dim.4
  10.1 12.0 %all-to-all-start = ((f32[32,1,64]{2,1,0:T(1,128)}), f32[32,1,64]{2,1,0:T(1,128)S(1)}, u32[]{:S(2)}, u32[]{:S(2)}) async-start(f32[32,1,64]{2,1,0:T(1,128)} %broadcast_in_dim.4), calls=%async_computation | async-start | bytes 32768 | tf_op jit(solution)/shard_map/all_to_all | solution.py:13
  22.1 0.1 multiply_reduce_fusion
  22.2 0.7 fusion.98
  23.0 7.8 %all-to-all-done = f32[32,1,64]{2,1,0:T(1,128)S(1)} async-done(((f32[32,1,64]{2,1,0:T(1,128)}), f32[32,1,64]{2,1,0:T(1,128)S(1)}, u32[]{:S(2)}, u32[]{:S(2)}) %all-to-all-start) | async-done | bytes 8224 | tf_op jit(solution)/shard_map/all_to_all | solution.py:13
  30.8 1.3 broadcast_in_dim.5
  32.0 6.4 %all-to-all-start.2 = ((s32[8,1,1]{2,1,0:T(1,128)}), s32[8,1,1]{2,1,0:T(1,128)S(1)}, u32[]{:S(2)}, u32[]{:S(2)}) async-start(s32[8,1,1]{2,1,0:T(1,128)} %broadcast_in_dim.5), calls=%async_computation.2 | async-start | bytes 8192 | tf_op jit(solution)/shard_map/all_to_all | solution.py:13
  38.4 0.6 broadcast.364
  39.0 0.7 reduce.12
  39.8 0.1 mul.343
  39.8 112.9 %all-gather.3.cloned.1.call-done = bf16[2048,4096]{1,0:T(8,128)(2,1)} async-done(((bf16[64,4096]{1,0:T(8,128)(2,1)}), bf16[2048,4096]{1,0:T(8,128)(2,1)}) %all-gather.3.cloned.1.call-update) | async-done | bytes 16777232 | tf_op jit(solution)/shard_map/all_gather | solution.py:54
  152.8 4.5 %fusion.9 = (f32[512]{0:T(512)S(1)}, f32[512]{0:T(512)S(1)}, f32[512]{0:T(512)S(1)}, f32[512]{0:T(512)S(1)}) fusion(bf16[2048,4096]{1,0:T(8,128)(2,1)} %all-gather.3.cloned.1.call-done), kind=kLoop, calls=%fused_computation.17 | loop fusion | flops 12580864 | bytes 8396800 | tf_op jit(solution)/shard_map/reduce_sum | solution.py:69
  157.3 2.7 %fusion.2 = bf16[2048,512]{1,0:T(8,128)(2,1)S(1)} fusion(f32[2048]{0:T(1024)S(1)} %mul.343, f32[512]{0:T(512)S(1)} %get-tuple-element.18, bf16[2048,4096]{1,0:T(8,128)(2,1)} %all-gather.3.cloned.1.call-done), kind=kLoop, calls=%fused_computation.10 | loop fusion | flops 4194304 | bytes 4204544 | tf_op jit(solution)/shard_map/convert_element_type | solution.py:70
  160.0 0.5 convolution_bitcast_fusion.6
  160.5 0.0 copy-start.6
  160.5 0.5 convolution_bitcast_fusion.7
  161.1 0.7 copy-done.1
  161.8 0.3 copy-done.6
  162.1 0.5 fusion.26
  162.6 0.8 fusion.63
  163.5 0.9 fusion.67
  164.4 0.7 convolution_bitcast_fusion.4
  165.1 0.7 convolution_bitcast_fusion.5
  165.8 0.7 convolution_bitcast_fusion.2
  166.6 0.7 convolution_bitcast_fusion.3
  167.3 0.7 convolution_bitcast_fusion
  168.0 0.7 convolution_bitcast_fusion.1
  168.7 0.5 fusion.25
  169.3 0.5 fusion.24
  169.8 0.5 fusion.23
  170.4 1.2 convolution_subtract_fusion.8
  171.6 1.2 convolution_subtract_fusion.7
  172.8 1.3 fusion.17
  174.1 0.2 copy.33
  174.3 0.1 copy.26
  174.4 1.1 convolution_subtract_fusion.5
  175.5 1.3 convolution_subtract_fusion.4
  176.9 1.2 fusion.16
  178.1 0.2 copy.34
  178.3 0.1 copy.27
  178.4 0.8 fusion.18
  179.2 0.9 convolution_subtract_fusion.2
  180.1 0.9 convolution_subtract_fusion.1
  181.0 1.0 fusion.15
  182.0 0.2 copy.35
  182.1 0.1 copy.28
  182.3 1.5 maximum_bitcast_fusion
  183.7 0.0 all-to-all-done.2
  183.7 5.6 %all-to-all-start.1 = ((bf16[8,3,160,256]{3,2,1,0:T(8,128)(2,1)}), bf16[8,3,160,256]{3,2,1,0:T(8,128)(2,1)S(1)}, u32[]{:S(2)}, u32[]{:S(2)}) async-start(bf16[8,3,160,256]{3,2,1,0:T(8,128)(2,1)} %maximum_bitcast_fusion), calls=%async_computation.1 | async-start | bytes 3932160 | tf_op jit(solution)/shard_map/all_to_all | solution.py:24
  189.4 0.7 reduce_sum.79
  190.8 23.4 %all-to-all-done.1 = bf16[8,3,160,256]{3,2,1,0:T(8,128)(2,1)S(1)} async-done(((bf16[8,3,160,256]{3,2,1,0:T(8,128)(2,1)}), bf16[8,3,160,256]{3,2,1,0:T(8,128)(2,1)S(1)}, u32[]{:S(2)}, u32[]{:S(2)}) %all-to-all-start.1) | async-done | bytes 1966112 | tf_op jit(solution)/shard_map/all_to_all | solution.py:24
  214.2 0.3 convert_reduce_fusion
  214.5 0.7 divide_convert_fusion
  215.2 0.0 all-gather.5.cloned.1.call-update
  215.2 25.0 %all-gather.5.cloned.1.call-done = bf16[3,160,2048]{2,1,0:T(8,128)(2,1)} async-done(((bf16[3,160,256]{2,1,0:T(8,128)(2,1)}), bf16[3,160,2048]{2,1,0:T(8,128)(2,1)}) %all-gather.5.cloned.1.call-update) | async-done | bytes 1966096 | tf_op jit(solution)/shard_map/all_gather | solution.py:81
  240.2 4.0 %convert_element_type.120 = f32[3,160,2048]{2,1,0:T(8,128)} convert(bf16[3,160,2048]{2,1,0:T(8,128)(2,1)} %all-gather.5.cloned.1.call-done) | non-fusion elementwise | flops 983040 | bytes 5898240 | tf_op jit(solution)/shard_map/convert_element_type | solution.py:81
  (15 shorter events, 0.1 us)
Async XLA Ops:
  6.5 153.5 %copy-start = (bf16[160,2048]{1,0:T(8,128)(2,1)S(1)}, bf16[160,2048]{1,0:T(8,128)(2,1)}, u32[]{:S(2)}) copy-start(bf16[160,2048]{1,0:T(8,128)(2,1)} %param.13) | copy-start | bytes 1966084
  6.5 2.9 %copy-start.5 = (f32[64]{0:T(128)S(1)}, f32[64]{0:T(128)}, u32[]{:S(2)}) copy-start(f32[64]{0:T(128)} %param.9) | copy-start | bytes 772
  6.5 15.6 %copy-start.4 = (s32[1,4,2]{1,2,0:T(2,128)S(1)}, s32[1,4,2]{1,2,0:T(2,128)}, u32[]{:S(2)}) copy-start(s32[1,4,2]{1,2,0:T(2,128)} %param.11) | copy-start | bytes 100
  6.5 15.7 %copy-start.3 = (s32[1,4,512]{2,1,0:T(4,128)S(1)}, s32[1,4,512]{2,1,0:T(4,128)}, u32[]{:S(2)}) copy-start(s32[1,4,512]{2,1,0:T(4,128)} %param.12) | copy-start | bytes 24580
  6.5 146.2 %all-gather.3.cloned.1.call-start = ((), (), s32[]{:S(2)}) async-start(), calls=%async_computation.3 | async-start | bytes 17301504 | tf_op jit(solution)/shard_map/all_gather | solution.py:54
  9.5 151.1 %copy-start.2 = (bf16[160,2048]{1,0:T(8,128)(2,1)S(1)}, bf16[160,2048]{1,0:T(8,128)(2,1)}, u32[]{:S(2)}) copy-start(bf16[160,2048]{1,0:T(8,128)(2,1)} %param.14) | copy-start | bytes 1966084
  10.1 20.7 %all-to-all-start = ((f32[32,1,64]{2,1,0:T(1,128)}), f32[32,1,64]{2,1,0:T(1,128)S(1)}, u32[]{:S(2)}, u32[]{:S(2)}) async-start(f32[32,1,64]{2,1,0:T(1,128)} %broadcast_in_dim.4), calls=%async_computation | async-start | bytes 32768 | tf_op jit(solution)/shard_map/all_to_all | solution.py:13
  32.0 151.7 %all-to-all-start.2 = ((s32[8,1,1]{2,1,0:T(1,128)}), s32[8,1,1]{2,1,0:T(1,128)S(1)}, u32[]{:S(2)}, u32[]{:S(2)}) async-start(s32[8,1,1]{2,1,0:T(1,128)} %broadcast_in_dim.5), calls=%async_computation.2 | async-start | bytes 8192 | tf_op jit(solution)/shard_map/all_to_all | solution.py:13
  152.8 9.0 %copy-start.1 = (bf16[2048,4096]{1,0:T(8,128)(2,1)S(1)}, bf16[2048,4096]{1,0:T(8,128)(2,1)}, u32[]{:S(2)}) copy-start(bf16[2048,4096]{1,0:T(8,128)(2,1)} %all-gather.3.cloned.1.call-done) | copy-start | bytes 50331652
  160.5 1.6 copy-start.6
  183.7 30.4 %all-to-all-start.1 = ((bf16[8,3,160,256]{3,2,1,0:T(8,128)(2,1)}), bf16[8,3,160,256]{3,2,1,0:T(8,128)(2,1)S(1)}, u32[]{:S(2)}, u32[]{:S(2)}) async-start(bf16[8,3,160,256]{3,2,1,0:T(8,128)(2,1)} %maximum_bitcast_fusion), calls=%async_computation.1 | async-start | bytes 3932160 | tf_op jit(solution)/shard_map/all_to_all | solution.py:24
  189.4 50.9 %all-gather.5.cloned.1.call-start = ((), (), s32[]{:S(2)}) async-start(), calls=%async_computation.4 | async-start | bytes 2211840 | tf_op jit(solution)/shard_map/all_gather | solution.py:81
Sparse Core Ops, SparseCore 0:
  9.9 142.7 all-gather.2
  215.3 24.8 all-gather.4
